TPU v7x, 32 devices: a whole 2x2x4 slice. The times are simulated.
32 devices in a mesh: grp: 4 (over z), dev: 8 (over y, x, core).
Axes of the slice: x: 2, y: 2, z: 4, core: 2. Of those that a mesh axis runs over, the one named last changes fastest.
Arguments:
- blocks: bfloat16 [4096, 128, 128], P(('grp', 'dev')), may hold values from -0.29882812 to 0.29882812
- ids_one: int32 [2, 4096], P(None, ('grp', 'dev')), may hold values from 0 to 255, as said below
- ids_two: int32 [2, 2048], P(None, ('grp', 'dev')), may hold values from 0 to 127, as said below
- ids_three: int32 [2, 1024], P(None, ('grp', 'dev')), may hold values from 0 to 63
- match_one: int32 [256, 128], replicated, may hold values from 0 to 127, as said below
- match_two: int32 [128, 128], replicated, may hold values from 0 to 127, as said below
- match_three: int32 [64, 128], replicated, may hold values from 0 to 127, as said below
- target_one: int32 [4096], P(('grp', 'dev')), may hold values from 0 to 63
- target_two: int32 [2048], P(('grp', 'dev')), may hold values from 0 to 31
- target_three: int32 [1024], P(('grp', 'dev')), may hold values from 0 to 15
- vertex_weights: float32 [256, 128], P(('grp', 'dev')), may hold values from 0.1 to 120, as said below
Outputs:
- coarse_graph: float32 [512, 128, 128], P(('grp', 'dev'))
- rel_weight: float32 [32, 128], P(('grp', 'dev'))
Inputs may be any that keep to these rules, and one draw needn't show every extreme that they name: `match_one`: rows 2b and 2b + 1 together name every number 0 to 127 exactly twice. `match_two`: rows 2b and 2b + 1 together name every number 0 to 127 exactly twice. `match_three`: rows 2b and 2b + 1 together name every number 0 to 127 exactly twice. `ids_one`: a fine block's row and column vertex blocks, halved by integer division, are the ids_two of the coarse slot it goes to. `ids_two`: a first-level block's row and column vertex blocks, halved by integer division, are the ids_three of the coarse slot it goes to. `vertex_weights`: positive.
All inputs are finite; a program needn't handle non-finite values.
Results may differ from a plain program's by a relative error of at most 0.0003.
Values may be sent and summed in bfloat16 or wider, within the bound.
A program may use at most 128 MiB of HBM per device.

v0:
```python
import math

import jax
import jax.numpy as jnp
from jax import lax
from jax.sharding import PartitionSpec as P


def project(blocks, pair_ids, table):
    row_map = table[pair_ids[0]]
    col_map = table[pair_ids[1]]
    count = blocks.shape[0]
    width = blocks.shape[1]
    group = math.gcd(count, 32)
    lanes = jnp.arange(width, dtype=jnp.int32)
    narrow = blocks.dtype == jnp.bfloat16

    def single(piece):
        block_part, rows_part, cols_part = piece
        right_hot = (cols_part[:, :, None] == lanes).astype(jnp.float32)
        if narrow:
            left_hot = (rows_part[:, :, None] == lanes).astype(jnp.bfloat16)
            halfway = jnp.einsum(
                "gim,gij->gmj", left_hot, block_part, preferred_element_type=jnp.float32
            )
        else:
            left_hot = (rows_part[:, :, None] == lanes).astype(jnp.float32)
            halfway = jnp.einsum(
                "gim,gij->gmj",
                left_hot,
                block_part,
                preferred_element_type=jnp.float32,
                precision=lax.Precision.HIGHEST,
            )
        return jnp.einsum(
            "gmj,gjn->gmn",
            halfway,
            right_hot,
            preferred_element_type=jnp.float32,
            precision=lax.Precision.HIGHEST,
        )

    pieces = (
        blocks.reshape(count // group, group, width, width),
        row_map.reshape(count // group, group, width),
        col_map.reshape(count // group, group, width),
    )
    return lax.map(single, pieces).reshape(count, width, width)


def gather_sum(received, targets, count):
    width = received.shape[1]
    hot = (jnp.arange(count, dtype=jnp.int32)[:, None] == targets[None, :]).astype(jnp.float32)
    flat = jnp.dot(
        hot,
        received.reshape(received.shape[0], width * width),
        preferred_element_type=jnp.float32,
        precision=lax.Precision.HIGHEST,
    )
    return flat.reshape(count, width, width)


def pair_weights(weights, table_rows):
    count, width = weights.shape
    lanes = jnp.arange(width, dtype=jnp.int32)
    hot = (table_rows.reshape(count // 2, 2 * width)[:, :, None] == lanes).astype(jnp.float32)
    return jnp.einsum(
        "kj,kjm->km",
        weights.reshape(count // 2, 2 * width),
        hot,
        preferred_element_type=jnp.float32,
        precision=lax.Precision.HIGHEST,
    )


def per_device(
    blocks,
    ids_one,
    ids_two,
    ids_three,
    match_one,
    match_two,
    match_three,
    target_one,
    target_two,
    target_three,
    vertex_weights,
):
    slots_zero = blocks.shape[0]
    labels = jnp.stack([ids_one[0], ids_one[1], target_one], axis=1)
    fine_in, labels_in = (
        lax.all_to_all(blocks, "dev", split_axis=0, concat_axis=0, tiled=True),
        lax.all_to_all(labels, "dev", split_axis=0, concat_axis=0, tiled=True),
    )
    received = project(fine_in, labels_in[:, :2].T, match_one)
    arrived = labels_in[:, 2]
    coarse_one = gather_sum(received, arrived, slots_zero // 2)
    parts_two = project(coarse_one, ids_two, match_two)
    received_two, arrived_two = (
        lax.all_to_all(parts_two, "dev", split_axis=0, concat_axis=0, tiled=True),
        lax.all_to_all(target_two, "dev", split_axis=0, concat_axis=0, tiled=True),
    )
    coarse_two = gather_sum(received_two, arrived_two, slots_zero // 4)
    parts_three = project(coarse_two, ids_three, match_three)
    received_three, arrived_three = (
        lax.all_to_all(parts_three, "grp", split_axis=0, concat_axis=0, tiled=True),
        lax.all_to_all(target_three, "grp", split_axis=0, concat_axis=0, tiled=True),
    )
    coarse_graph = gather_sum(received_three, arrived_three, slots_zero // 8)
    total = lax.psum(jnp.sum(vertex_weights), ("grp", "dev"))
    owned = vertex_weights.shape[0]
    position = lax.axis_index(("grp", "dev"))
    rows_one = lax.dynamic_slice_in_dim(match_one, position * owned, owned, 0)
    weights_one = pair_weights(vertex_weights, rows_one)
    rows_two = lax.dynamic_slice_in_dim(match_two, position * (owned // 2), owned // 2, 0)
    weights_two = pair_weights(weights_one, rows_two)
    rows_three = lax.dynamic_slice_in_dim(match_three, position * (owned // 4), owned // 4, 0)
    weights_three = pair_weights(weights_two, rows_three)
    vertices = weights_three.shape[0] * lax.axis_size(("grp", "dev")) * weights_three.shape[1]
    rel_weight = weights_three * vertices / total
    return (coarse_graph, rel_weight)


def solution(mesh):
    return jax.shard_map(
        per_device,
        mesh=mesh,
        in_specs=(
            P(("grp", "dev"), None, None),
            P(None, ("grp", "dev")),
            P(None, ("grp", "dev")),
            P(None, ("grp", "dev")),
            P(),
            P(),
            P(),
            P(("grp", "dev")),
            P(("grp", "dev")),
            P(("grp", "dev")),
            P(("grp", "dev"), None),
        ),
        out_specs=(P(("grp", "dev"), None, None), P(("grp", "dev"), None)),
        check_vma=False,
    )
```

profile of v0, /device:TPU:11, one launch (start us, length us, event | category | flops | bytes accessed | tf_op | source)
XLA Modules:
  0.0 284.9 jit_solution(8036044374910287233)
XLA Ops:
  0.6 0.8 slice_reduce_fusion.1
  1.6 0.7 stack.12
  2.3 7.6 %all_to_all.42 = s32[8,16,3]{1,2,0:T(4,128)S(1)} all-to-all(s32[8,16,3]{1,2,0:T(4,128)S(1)} %copy.34), channel_id=1, replica_groups=mesh['grp'=4,'dev'=8] {'dev'}, dimensions={0} | all-to-all | bytes 3072 | tf_op jit(solution)/shard_map/all_to_all | solution.py:93
  9.9 6.1 %all-to-all-start.3 = ((bf16[128,128,128]{2,1,0:T(8,128)(2,1)}), bf16[128,128,128]{2,1,0:T(8,128)(2,1)}, u32[]{:S(2)}, u32[]{:S(2)}) async-start(bf16[128,128,128]{2,1,0:T(8,128)(2,1)} %param.15), calls=%async_computation.3 | async-start | bytes 8388608 | tf_op jit(solution)/shard_map/all_to_all | solution.py:92
  16.1 0.6 gather_fusion.4
  16.7 0.6 gather_fusion.1
  17.3 0.7 all_to_all.29
  18.1 0.6 gather_fusion.2
  18.7 0.6 gather_fusion.3
  19.4 44.3 %all-to-all-done.3 = bf16[128,128,128]{2,1,0:T(8,128)(2,1)} async-done(((bf16[128,128,128]{2,1,0:T(8,128)(2,1)}), bf16[128,128,128]{2,1,0:T(8,128)(2,1)}, u32[]{:S(2)}, u32[]{:S(2)}) %all-to-all-start.3) | async-done | bytes 4194336 | tf_op jit(solution)/shard_map/all_to_all | solution.py:92
  63.7 4.8 %all-to-all-start.1 = ((s32[8,8,1]{1,2,0:T(1,128)}), s32[8,8,1]{1,2,0:T(1,128)S(1)}, u32[]{:S(2)}, u32[]{:S(2)}) async-start(s32[8,8,1]{1,2,0:T(1,128)} %bitcast.4), calls=%async_computation.1 | async-start | bytes 8192 | tf_op jit(solution)/shard_map/all_to_all | solution.py:101
  68.5 20.9 %while.28 = (s32[]{:T(128)}, f32[4,32,128,128]{3,2,1,0:T(8,128)}, s32[4,32,128]{2,1,0:T(8,128)S(1)}, bf16[4,32,128,128]{3,2,1,0:T(8,128)(2,1)}, s32[4,32,128]{2,1,0:T(8,128)S(1)}, /*index=5*/s32[]{:T(128)}) while((s32[]{:T(128)}, f32[4,32,128,128]{3,2,1,0:T(8,128)}, s32[4,32,128]{2,1,0:T(8,128)S(1)}, ...), condition=%wide.region_1.2_spmd.clone.clone, body=%wide.region_0.1_spmd.clone.clone.sunk | while | flops 940572672 | bytes 7439433 | solution.py:48
  68.5 2.6 fusion.66
  71.1 2.7 bitcast_dynamic-update-slice_fusion.4
  73.7 2.6 fusion.66
  76.3 2.6 bitcast_dynamic-update-slice_fusion.4
  79.0 2.6 fusion.66
  81.5 2.7 bitcast_dynamic-update-slice_fusion.4
  84.2 2.6 fusion.66
  86.7 2.7 bitcast_dynamic-update-slice_fusion.4
  89.4 13.2 %copy.74 = f32[16,8,128,128]{3,1,2,0:T(8,128)} copy(f32[16,8,128,128]{3,2,1,0:T(8,128)} %bitcast.158) | data formatting | bytes 16777216
  102.6 9.0 %copy.36 = f32[16384,128]{1,0:T(8,128)} copy(f32[16384,128]{0,1:T(8,128)} %bitcast.157) | data formatting | bytes 16777216 | tf_op jit(solution)/shard_map/dot_general | solution.py:54
  111.6 10.4 %fusion.35 = f32[2,32,128,128]{3,1,2,0:T(8,128)} fusion(f32[128,128,128,1]{2,1,0,3:T(8,128)} %bitcast.156, s32[128]{0:T(128)S(1)} %slice_bitcast_fusion.1, s32[2,32]{1,0:T(2,128)S(1)} %multiply_add_fusion), kind=kOutput, calls=%fused_computation.60 | convolution fusion | flops 1610620928 | bytes 12583680 | tf_op jit(solution)/shard_map/dot_general | solution.py:54
  121.9 17.3 %while.29 = (s32[]{:T(128)}, f32[2,32,128,128]{3,2,1,0:T(8,128)}, s32[2,32,128]{2,1,0:T(8,128)S(1)}, f32[2,32,128,128]{3,1,2,0:T(8,128)}, s32[2,32,128]{2,1,0:T(8,128)S(1)}, /*index=5*/s32[]{:T(128)}) while((s32[]{:T(128)}, f32[2,32,128,128]{3,2,1,0:T(8,128)}, s32[2,32,128]{2,1,0:T(8,128)S(1)}, ...), condition=%wide.region_3.4_spmd.clone.clone, body=%wide.region_2.3_spmd.clone.clone.sunk | while | flops 1611661312 | bytes 12681805 | solution.py:48
  122.0 1.8 constant_dynamic-slice_fusion.4
  123.7 4.2 %fusion.68 = f32[32,128,128]{2,1,0:T(8,128)S(1)} fusion(f32[1,32,128,128]{3,1,2,0:T(8,128)S(1)} %constant_dynamic-slice_fusion.4, s32[32,128]{1,0:T(8,128)S(1)} %get-tuple-element.280), kind=kOutput, calls=%fused_computation.23.clone.1 | convolution fusion | flops 805830656 | bytes 4210688 | tf_op jit(solution)/shard_map/while/body/eval_jaxpr/gim,gij->gmj/dot_general | solution.py:28
  127.9 2.7 bitcast_dynamic-update-slice_fusion.5
  130.6 1.8 constant_dynamic-slice_fusion.4
  132.4 4.2 %fusion.68 = f32[32,128,128]{2,1,0:T(8,128)S(1)} fusion(f32[1,32,128,128]{3,1,2,0:T(8,128)S(1)} %constant_dynamic-slice_fusion.4, s32[32,128]{1,0:T(8,128)S(1)} %get-tuple-element.280), kind=kOutput, calls=%fused_computation.23.clone.1 | convolution fusion | flops 805830656 | bytes 4210688 | tf_op jit(solution)/shard_map/while/body/eval_jaxpr/gim,gij->gmj/dot_general | solution.py:28
  136.6 2.6 bitcast_dynamic-update-slice_fusion.5
  139.3 4.7 %all-to-all-start.4 = ((f32[64,128,128]{2,1,0:T(8,128)}), f32[64,128,128]{2,1,0:T(8,128)}, u32[]{:S(2)}, u32[]{:S(2)}) async-start(f32[64,128,128]{2,1,0:T(8,128)} %bitcast.26), calls=%async_computation.4 | async-start | bytes 8388608 | tf_op jit(solution)/shard_map/all_to_all | solution.py:100
  144.0 0.6 gather_fusion
  144.6 0.6 gather_fusion.5
  145.2 0.7 all_to_all.27
  145.9 0.6 broadcast.197
  146.4 0.7 reduce.14
  147.2 44.4 %all-to-all-done.4 = f32[64,128,128]{2,1,0:T(8,128)} async-done(((f32[64,128,128]{2,1,0:T(8,128)}), f32[64,128,128]{2,1,0:T(8,128)}, u32[]{:S(2)}, u32[]{:S(2)}) %all-to-all-start.4) | async-done | bytes 4194336 | tf_op jit(solution)/shard_map/all_to_all | solution.py:100
  191.6 4.8 %all-to-all-start = ((s32[4,8,1]{1,2,0:T(1,128)}), s32[4,8,1]{1,2,0:T(1,128)S(1)}, u32[]{:S(2)}, u32[]{:S(2)}) async-start(s32[4,8,1]{1,2,0:T(1,128)} %bitcast), calls=%async_computation | async-start | bytes 4096 | tf_op jit(solution)/shard_map/all_to_all | solution.py:107
  196.4 6.1 %fusion.15 = f32[32,128,128]{2,0,1:T(8,128)S(1)} fusion(s32[64]{0:T(128)S(1)} %eq.224, f32[8,8,128,128]{3,2,1,0:T(8,128)} %bitcast.64), kind=kOutput, calls=%fused_computation.33 | convolution fusion | flops 402655232 | bytes 6291712 | tf_op jit(solution)/shard_map/dot_general | solution.py:54
  202.5 2.6 fusion.21
  205.1 2.7 fusion.23
  207.8 4.7 %all-to-all-start.5 = ((f32[32,128,128]{2,1,0:T(8,128)}), f32[32,128,128]{2,1,0:T(8,128)S(1)}, u32[]{:S(2)}, u32[]{:S(2)}) async-start(f32[32,128,128]{2,1,0:T(8,128)} %fusion.23), calls=%async_computation.5 | async-start | bytes 4194304 | tf_op jit(solution)/shard_map/all_to_all | solution.py:106
  212.4 0.6 reduce_sum.9
  213.0 65.6 %psum.7 = f32[]{:T(128)} all-reduce(f32[]{:T(128)} %reduce_sum.9), channel_id=1, replica_groups=mesh['grp'=4,'dev'=8] {'grp','dev'}, use_global_device_ids=true, to_apply=%region_5.6 | all-reduce | flops 1 | bytes 8 | tf_op jit(solution)/shard_map/psum | solution.py:110
  279.4 1.4 fusion.26
  280.8 0.7 reduce.15
  281.6 2.0 fusion.18
  283.6 1.3 copy.41
  (52 shorter events, 1.3 us)
Async XLA Ops:
  0.6 17.5 %copy-start = (s32[256,128]{1,0:T(8,128)S(1)}, s32[256,128]{1,0:T(8,128)}, u32[]{:S(2)}) copy-start(s32[256,128]{1,0:T(8,128)} %param.19) | copy-start | bytes 393220
  9.9 6.1 %copy-start.4 = (s32[2,64]{1,0:T(2,128)S(1)}, s32[2,64]{1,0:T(2,128)}, u32[]{:S(2)}) copy-start(s32[2,64]{1,0:T(2,128)} %param.17) | copy-start | bytes 1540
  9.9 6.2 %copy-start.1 = (s32[128,128]{1,0:T(8,128)S(1)}, s32[128,128]{1,0:T(8,128)}, u32[]{:S(2)}) copy-start(s32[128,128]{1,0:T(8,128)} %param.20) | copy-start | bytes 196612
  9.9 7.4 %copy-start.6 = (s32[64]{0:T(128)S(1)}, s32[64]{0:T(128)}, u32[]{:S(2)}) copy-start(s32[64]{0:T(128)} %param.23) | copy-start | bytes 772
  9.9 53.8 %all-to-all-start.3 = ((bf16[128,128,128]{2,1,0:T(8,128)(2,1)}), bf16[128,128,128]{2,1,0:T(8,128)(2,1)}, u32[]{:S(2)}, u32[]{:S(2)}) async-start(bf16[128,128,128]{2,1,0:T(8,128)(2,1)} %param.15), calls=%async_computation.3 | async-start | bytes 8388608 | tf_op jit(solution)/shard_map/all_to_all | solution.py:92
  63.7 75.6 %all-to-all-start.1 = ((s32[8,8,1]{1,2,0:T(1,128)}), s32[8,8,1]{1,2,0:T(1,128)S(1)}, u32[]{:S(2)}, u32[]{:S(2)}) async-start(s32[8,8,1]{1,2,0:T(1,128)} %bitcast.4), calls=%async_computation.1 | async-start | bytes 8192 | tf_op jit(solution)/shard_map/all_to_all | solution.py:101
  139.3 4.7 %copy-start.5 = (s32[2,32]{1,0:T(2,128)S(1)}, s32[2,32]{1,0:T(2,128)}, u32[]{:S(2)}) copy-start(s32[2,32]{1,0:T(2,128)} %param.18) | copy-start | bytes 772
  139.3 4.7 %copy-start.2 = (s32[64,128]{1,0:T(8,128)S(1)}, s32[64,128]{1,0:T(8,128)}, u32[]{:S(2)}) copy-start(s32[64,128]{1,0:T(8,128)} %param.21) | copy-start | bytes 98308
  139.3 5.9 %copy-start.7 = (s32[32]{0:T(128)S(1)}, s32[32]{0:T(128)}, u32[]{:S(2)}) copy-start(s32[32]{0:T(128)} %param.24) | copy-start | bytes 388
  139.3 52.3 %all-to-all-start.4 = ((f32[64,128,128]{2,1,0:T(8,128)}), f32[64,128,128]{2,1,0:T(8,128)}, u32[]{:S(2)}, u32[]{:S(2)}) async-start(f32[64,128,128]{2,1,0:T(8,128)} %bitcast.26), calls=%async_computation.4 | async-start | bytes 8388608 | tf_op jit(solution)/shard_map/all_to_all | solution.py:100
  191.6 16.1 %all-to-all-start = ((s32[4,8,1]{1,2,0:T(1,128)}), s32[4,8,1]{1,2,0:T(1,128)S(1)}, u32[]{:S(2)}, u32[]{:S(2)}) async-start(s32[4,8,1]{1,2,0:T(1,128)} %bitcast), calls=%async_computation | async-start | bytes 4096 | tf_op jit(solution)/shard_map/all_to_all | solution.py:107
  207.8 4.7 %copy-start.3 = (f32[8,128]{1,0:T(8,128)S(1)}, f32[8,128]{1,0:T(8,128)}, u32[]{:S(2)}) copy-start(f32[8,128]{1,0:T(8,128)} %param.25) | copy-start | bytes 12292
  207.8 73.8 %all-to-all-start.5 = ((f32[32,128,128]{2,1,0:T(8,128)}), f32[32,128,128]{2,1,0:T(8,128)S(1)}, u32[]{:S(2)}, u32[]{:S(2)}) async-start(f32[32,128,128]{2,1,0:T(8,128)} %fusion.23), calls=%async_computation.5 | async-start | bytes 4194304 | tf_op jit(solution)/shard_map/all_to_all | solution.py:106
where the time goes:
time: 289 us; the launch traced here: 285 us
  waiting for transfers between devices  88.7 us (31%)
  blocking collectives  73.2 us (25%)
  matrix products  60.4 us (21%)
  local copies, waits for them, and re-layouts  34.5 us (12%)
  starting transfers between devices  25.1 us (9%)
    psum x1, blocking collectives, per_device(): total = lax.psum(jnp.sum(vertex_weights), ('grp', 'dev'))  65.6 us
    all_to_all x1, waiting for transfers between devices, per_device(): lax.all_to_all(parts_two, 'dev', split_axis=0, concat_axis=0, tiled=True)  44.4 us
    all_to_all x1, waiting for transfers between devices, per_device(): lax.all_to_all(blocks, 'dev', split_axis=0, concat_axis=0, tiled=True)  44.3 us
    dot_general x7, matrix products, single(): jnp.einsum('gim,gij->gmj', left_hot, block_part, preferred_element_type=j...  21.3 us
    dot_general x7, matrix products, single(): jnp.einsum('gmj,gjn->gmn', halfway, right_hot, preferred_element_type=jnp...  18.7 us
    dot_general x3, matrix products, gather_sum(): jnp.dot(hot, received.reshape(received.shape[0], width * width), preferre...  18.4 us
    unnamed x18, local copies, waits for them, and re-layouts  14.5 us
    dot_general x1, local copies, waits for them, and re-layouts, gather_sum(): jnp.dot(hot, received.reshape(received.shape[0], width * width), preferre...  9 us
  transfers between devices with their start and end apart: 5, of which 2 were waited for; matrix products, arithmetic and copies ran while one was open for 32% of the time, Pallas kernels for 0%

commit v1 on v0

v1 whole, which is shorter than its diff:
```python
import functools

import jax
import jax.numpy as jnp
from jax import lax
from jax.experimental import pallas as pl
from jax.experimental.pallas import tpu as pltpu
from jax.sharding import PartitionSpec as P

LEVELS = 32767.0
TINY = 1e-30
NT = (((1,), (1,)), ((), ()))


def hot(row, width):
    names = lax.broadcasted_iota(jnp.int32, (width, width), 0)
    return (names == row).astype(jnp.bfloat16)


def halves(x):
    high = x.astype(jnp.bfloat16)
    low = (x - high.astype(jnp.float32)).astype(jnp.bfloat16)
    return high, low


def columns(halfway, col):
    width = col.shape[1]
    right = hot(col, width)
    left = jnp.concatenate(halves(halfway), axis=1)
    both = jnp.concatenate([right, right], axis=1)
    return lax.dot_general(left, both, NT, preferred_element_type=jnp.float32)


def project_narrow(block, row, col):
    left = hot(row, row.shape[1])
    return columns(jnp.dot(left, block, preferred_element_type=jnp.float32), col)


def project_wide(block, row, col):
    left = hot(row, row.shape[1])
    both = jnp.concatenate([left, left], axis=1)
    stacked = jnp.concatenate(halves(block), axis=0)
    return columns(jnp.dot(both, stacked, preferred_element_type=jnp.float32), col)


def encode(part):
    peak = jnp.maximum(jnp.max(jnp.abs(part), axis=0, keepdims=True), TINY)
    code = jnp.round(part * (LEVELS / peak)).astype(jnp.int32)
    return code.astype(jnp.int16), peak * (1.0 / LEVELS)


def decode(code, scale):
    return code.astype(jnp.int32).astype(jnp.float32) * scale


def level_one(chunk, labels, ids, table, next_table, blocks, codes, scales, total):
    step = pl.program_id(0)

    @pl.when(step == 0)
    def _():
        total[...] = jnp.zeros_like(total)

    def several(start, count):
        parts = []
        for j in range(count):
            k = step * chunk + start + j
            row = table[pl.ds(labels[0, k], 1), :]
            col = table[pl.ds(labels[1, k], 1), :]
            parts.append(project_narrow(blocks[start + j], row, col))
        for j in range(count):
            k = step * chunk + start + j
            total[labels[2, k]] += parts[j]

    unroll = 4
    pl.loop(0, chunk // unroll)(lambda i: several(i * unroll, unroll))

    @pl.when(step == pl.num_programs(0) - 1)
    def _():
        send_parts(total, ids, next_table, codes, scales)


def send_parts(total, ids, table, codes, scales):
    unroll = 4

    def several(i):
        for j in range(unroll):
            k = i * unroll + j
            row = table[pl.ds(ids[0, k], 1), :]
            col = table[pl.ds(ids[1, k], 1), :]
            code, scale = encode(project_wide(total[k], row, col))
            codes[k] = code
            scales[k] = scale

    pl.loop(0, total.shape[0] // unroll)(several)


def level_two(targets, ids, table, codes_in, scales_in, codes, scales, total):
    total[...] = jnp.zeros_like(total)

    @pl.loop(0, codes_in.shape[0])
    def _(k):
        total[targets[k]] += decode(codes_in[k], scales_in[k])

    send_parts(total, ids, table, codes, scales)


def level_three(targets, codes_in, scales_in, total):
    total[...] = jnp.zeros_like(total)

    @pl.loop(0, codes_in.shape[0])
    def _(k):
        total[targets[k]] += decode(codes_in[k], scales_in[k])


SMEM = pl.BlockSpec(memory_space=pltpu.SMEM)
VMEM = pl.BlockSpec(memory_space=pltpu.VMEM)
PARAMS = pltpu.CompilerParams(vmem_limit_bytes=56 * 1024 * 1024)


def coded(count, width):
    return (
        jax.ShapeDtypeStruct((count, width, width), jnp.int16),
        jax.ShapeDtypeStruct((count, 1, width), jnp.float32),
    )


def pair_weights(weights, table_rows):
    count, width = weights.shape
    lanes = jnp.arange(width, dtype=jnp.int32)
    match = table_rows.reshape(count // 2, 2 * width)[:, :, None] == lanes
    spread = weights.reshape(count // 2, 2 * width)[:, :, None]
    return jnp.sum(jnp.where(match, spread, 0.0), axis=1)


def per_device(
    blocks,
    ids_one,
    ids_two,
    ids_three,
    match_one,
    match_two,
    match_three,
    target_one,
    target_two,
    target_three,
    vertex_weights,
):
    swap = functools.partial(lax.all_to_all, split_axis=0, concat_axis=0, tiled=True)
    count, width = blocks.shape[0], blocks.shape[1]
    labels = swap(jnp.stack([ids_one[0], ids_one[1], target_one], axis=1), "dev").T
    arrived_two = swap(target_two, "dev")
    arrived_three = swap(target_three, "grp")
    blocks = swap(blocks, "dev")
    chunk = 16
    codes, scales = pl.pallas_call(
        functools.partial(level_one, chunk),
        grid=(count // chunk,),
        in_specs=[
            SMEM,
            SMEM,
            VMEM,
            VMEM,
            pl.BlockSpec((chunk, width, width), lambda i: (i, 0, 0)),
        ],
        out_specs=(VMEM, VMEM),
        out_shape=coded(count // 2, width),
        scratch_shapes=[pltpu.VMEM((count // 2, width, width), jnp.float32)],
        compiler_params=PARAMS,
    )(labels, ids_two, match_one, match_two, blocks)
    codes, scales = swap(codes, "dev"), swap(scales, "dev")
    codes, scales = pl.pallas_call(
        level_two,
        in_specs=[SMEM, SMEM, VMEM, VMEM, VMEM],
        out_specs=(VMEM, VMEM),
        out_shape=coded(count // 4, width),
        scratch_shapes=[pltpu.VMEM((count // 4, width, width), jnp.float32)],
        compiler_params=PARAMS,
    )(arrived_two, ids_three, match_three, codes, scales)
    codes, scales = swap(codes, "grp"), swap(scales, "grp")
    coarse_graph = pl.pallas_call(
        level_three,
        in_specs=[SMEM, VMEM, VMEM],
        out_specs=VMEM,
        out_shape=jax.ShapeDtypeStruct((count // 8, width, width), jnp.float32),
        compiler_params=PARAMS,
    )(arrived_three, codes, scales)

    sums = lax.all_gather(jnp.sum(vertex_weights).reshape(1), ("grp", "dev"), tiled=True)
    total = jnp.sum(sums)
    owned = vertex_weights.shape[0]
    position = lax.axis_index(("grp", "dev"))
    weights = vertex_weights
    for table in (match_one, match_two, match_three):
        rows = lax.dynamic_slice_in_dim(table, position * owned, owned, 0)
        weights = pair_weights(weights, rows)
        owned //= 2
    vertices = weights.shape[0] * lax.axis_size(("grp", "dev")) * weights.shape[1]
    return coarse_graph, weights * vertices / total


def solution(mesh):
    both = ("grp", "dev")
    return jax.shard_map(
        per_device,
        mesh=mesh,
        in_specs=(
            P(both, None, None),
            P(None, both),
            P(None, both),
            P(None, both),
            P(),
            P(),
            P(),
            P(both),
            P(both),
            P(both),
            P(both, None),
        ),
        out_specs=(P(both, None, None), P(both, None)),
        check_vma=False,
    )
```

time: 289 us -> 212 us (0.73)
  matrix products: 60.4 us -> 0 us
  Pallas kernels: 0 us -> 34.3 us
  local copies, waits for them, and re-layouts: 34.5 us -> 9.33 us
  waiting for transfers between devices: 88.7 us -> 68.9 us
  blocking collectives: 73.2 us -> 65.4 us
    psum x1 -> x0, blocking collectives: 65.6 us -> none  [per_device(): total = lax.psum(jnp.sum(vertex_weights), ('grp', 'dev'))]
    dot_general x20 -> x0, matrix products: 60.4 us -> none  [the longest x7 21.3 us: single(): jnp.einsum('gim,gij->gmj', left_hot, block_part, preferred_element_type=j...]
    unnamed x0 -> x1, blocking collectives: none -> 42.2 us
    pallas_call x0 -> x3, Pallas kernels: none -> 34.3 us  [the longest x1 24.8 us: per_device(): pl.pallas_call(functools.partial(level_one, chunk), grid=(count // chunk,...]
    all_to_all x5, waiting for transfers between devices: 88.7 us -> 68.9 us  [the longest x1 46.3 us: per_device(): blocks = swap(blocks, 'dev')]
    all_to_all x1 -> x3, blocking collectives: 7.58 us -> 23.2 us  [the longest x1 8 us: per_device(): codes, scales = (swap(codes, 'grp'), swap(scales, 'grp'))]
    unnamed x18 -> x12, local copies, waits for them, and re-layouts: 14.5 us -> 1.76 us
    dot_general x1 -> x0, local copies, waits for them, and re-layouts: 9 us -> none  [gather_sum(): jnp.dot(hot, received.reshape(received.shape[0], width * width), preferre...]
  transfers between devices with their start and end apart: 5 -> 5, of which waited for: 2 -> 2; matrix products, arithmetic and copies ran while one was open for 32% -> 4% of each run, Pallas kernels for 0% -> 15%
where the time goes in v1:
time: 212 us; the launch traced here: 208 us
  waiting for transfers between devices  68.9 us (33%)
  blocking collectives  65.4 us (31%)
  Pallas kernels  34.3 us (16%)
  starting transfers between devices  25.4 us (12%)
  local copies, waits for them, and re-layouts  9.33 us (4%)
  other arithmetic  4.48 us (2%)
    all_to_all x1, waiting for transfers between devices, per_device(): blocks = swap(blocks, 'dev')  46.3 us
    unnamed x1, blocking collectives  42.2 us
    pallas_call x1, Pallas kernels, per_device(): pl.pallas_call(functools.partial(level_one, chunk), grid=(count // chunk,...  24.8 us
    all_to_all x1, waiting for transfers between devices, per_device(): codes, scales = (swap(codes, 'dev'), swap(scales, 'dev'))  22.6 us
    all_to_all x1, blocking collectives, per_device(): codes, scales = (swap(codes, 'grp'), swap(scales, 'grp'))  8 us
    all_to_all x1, blocking collectives, per_device(): codes, scales = (swap(codes, 'dev'), swap(scales, 'dev'))  7.62 us
    all_to_all x1, blocking collectives, per_device(): swap(jnp.stack([ids_one[0], ids_one[1], target_one], axis=1), 'dev')  7.58 us
    pallas_call x1, Pallas kernels, per_device(): pl.pallas_call(level_two, in_specs=[SMEM, SMEM, VMEM, VMEM, VMEM], out_sp...  6.85 us
  transfers between devices with their start and end apart: 5, of which 2 were waited for; matrix products, arithmetic and copies ran while one was open for 4% of the time, Pallas kernels for 15%

profile of v1, /device:TPU:11, one launch (start us, length us, event | category | flops | bytes accessed | tf_op | source)
XLA Modules:
  0.0 208.4 jit_solution(417916673680621502)
XLA Ops:
  0.6 0.8 slice_reduce_fusion.1
  1.4 0.1 stack.10
  1.5 0.1 stack.11
  1.6 0.7 stack.12
  2.3 7.6 %all_to_all.56 = s32[8,16,3]{1,2,0:T(4,128)S(1)} all-to-all(s32[8,16,3]{1,2,0:T(4,128)S(1)} %copy.19), channel_id=1, replica_groups=mesh['grp'=4,'dev'=8] {'dev'}, dimensions={0} | all-to-all | bytes 3072 | tf_op jit(solution)/shard_map/all_to_all | solution.py:150
  9.9 0.0 copy-start.3
  9.9 6.1 %all-to-all-start.3 = ((bf16[128,128,128]{2,1,0:T(8,128)(2,1)}), bf16[128,128,128]{2,1,0:T(8,128)(2,1)}, u32[]{:S(2)}, u32[]{:S(2)}) async-start(bf16[128,128,128]{2,1,0:T(8,128)(2,1)} %param.11), calls=%async_computation.3 | async-start | bytes 8388608 | tf_op jit(solution)/shard_map/all_to_all | solution.py:153
  16.0 0.0 copy-done.3
  16.0 0.7 all_to_all.38
  16.7 0.7 all_to_all.42
  17.3 46.3 %all-to-all-done.3.blocks = bf16[128,128,128]{2,1,0:T(8,128)(2,1)} async-done(((bf16[128,128,128]{2,1,0:T(8,128)(2,1)}), bf16[128,128,128]{2,1,0:T(8,128)(2,1)}, u32[]{:S(2)}, u32[]{:S(2)}) %all-to-all-start.3) | async-done | bytes 4194336 | tf_op jit(solution)/shard_map/all_to_all | solution.py:153
  63.6 4.8 %all-to-all-start.1 = ((s32[8,8,1]{1,2,0:T(1,128)}), s32[8,8,1]{1,2,0:T(1,128)S(1)}, u32[]{:S(2)}, u32[]{:S(2)}) async-start(s32[8,8,1]{1,2,0:T(1,128)} %bitcast.1), calls=%async_computation.1 | async-start | bytes 8192 | tf_op jit(solution)/shard_map/all_to_all | solution.py:151
  68.4 0.0 copy-start.4
  68.4 24.8 %shard_map.122 = (s16[64,128,128]{2,1,0:T(8,128)(2,1)}, f32[64,1,128]{2,1,0:T(1,128)}) custom-call(s32[3,128]{1,0:T(4,128)} %bitcast.13, s32[2,64]{1,0:T(2,128)} %ids.2, s32[256,128]{1,0:T(8,128)} %table.2, s32[128,128]{1,0:T(8,128)} %next_table.1, bf16[128,128,128]{2,1,0:T(8,128)(2,1)} %all-to-all-done.3.blocks), custom_call_target="tpu_custom_call" | custom-call | tf_op jit(solution)/shard_map/pallas_call | solution.py:155
  93.1 0.0 all-to-all-done.1
  93.1 7.6 %all_to_all.57.scales_in = f32[64,1,128]{2,1,0:T(1,128)} all-to-all(f32[64,1,128]{2,1,0:T(1,128)} %get-tuple-element.7), channel_id=1, replica_groups=mesh['grp'=4,'dev'=8] {'dev'}, dimensions={0} | all-to-all | bytes 65536 | tf_op jit(solution)/shard_map/all_to_all | solution.py:170
  100.8 0.0 copy-start.2
  100.8 5.2 %all-to-all-start.4 = ((s16[64,128,128]{2,1,0:T(8,128)(2,1)}), s16[64,128,128]{2,1,0:T(8,128)(2,1)S(1)}, u32[]{:S(2)}, u32[]{:S(2)}) async-start(s16[64,128,128]{2,1,0:T(8,128)(2,1)} %get-tuple-element.6), calls=%async_computation.4 | async-start | bytes 4194304 | tf_op jit(solution)/shard_map/all_to_all | solution.py:170
  106.0 0.0 copy-done.4
  106.0 0.7 all_to_all.35
  106.6 0.6 broadcast.80
  107.2 0.6 reduce.17
  107.8 0.6 all_to_all.40.targets
  108.4 22.6 %all-to-all-done.4.codes_in = s16[64,128,128]{2,1,0:T(8,128)(2,1)S(1)} async-done(((s16[64,128,128]{2,1,0:T(8,128)(2,1)}), s16[64,128,128]{2,1,0:T(8,128)(2,1)S(1)}, u32[]{:S(2)}, u32[]{:S(2)}) %all-to-all-start.4) | async-done | bytes 2097184 | tf_op jit(solution)/shard_map/all_to_all | solution.py:170
  131.0 0.0 copy-start
  131.0 4.8 %all-to-all-start = ((s32[4,8,1]{1,2,0:T(1,128)}), s32[4,8,1]{1,2,0:T(1,128)S(1)}, u32[]{:S(2)}, u32[]{:S(2)}) async-start(s32[4,8,1]{1,2,0:T(1,128)} %bitcast), calls=%async_computation | async-start | bytes 4096 | tf_op jit(solution)/shard_map/all_to_all | solution.py:152
  135.8 0.0 copy-done
  135.8 6.9 %shard_map.123 = (s16[32,128,128]{2,1,0:T(8,128)(2,1)}, f32[32,1,128]{2,1,0:T(1,128)}) custom-call(s32[64]{0:T(128)} %all_to_all.40.targets, s32[2,32]{1,0:T(2,128)} %ids.3, s32[64,128]{1,0:T(8,128)} %table.3, s16[64,128,128]{2,1,0:T(8,128)(2,1)} %copy-done, f32[64,1,128]{2,1,0:T(1,128)} %all_to_all.57.scales_in), custom_call_target="tpu_custom_call" | custom-call | tf_op jit(solution)/shard_map/pallas_call | solution.py:171
  142.7 0.0 all-to-all-done
  142.7 8.0 %all_to_all.58.scales_in = f32[32,1,128]{2,1,0:T(1,128)} all-to-all(f32[32,1,128]{2,1,0:T(1,128)} %get-tuple-element.9), channel_id=1, replica_groups=mesh['grp'=4,'dev'=8] {'grp'}, dimensions={0} | all-to-all | bytes 32768 | tf_op jit(solution)/shard_map/all_to_all | solution.py:179
  150.7 4.6 %all-to-all-start.6 = ((s16[32,128,128]{2,1,0:T(8,128)(2,1)}), s16[32,128,128]{2,1,0:T(8,128)(2,1)S(1)}, u32[]{:S(2)}, u32[]{:S(2)}) async-start(s16[32,128,128]{2,1,0:T(8,128)(2,1)} %get-tuple-element.8), calls=%async_computation.6 | async-start | bytes 2097152 | tf_op jit(solution)/shard_map/all_to_all | solution.py:179
  155.2 0.0 copy-done.2
  155.2 0.6 reduce_sum.48
  155.8 0.8 dynamic-update-slice
  156.6 42.2 %all-reduce = f32[32]{0:T(128)S(1)} all-reduce(f32[32]{0:T(128)S(1)} %dynamic-update-slice), channel_id=1, replica_groups=mesh['grp'=4,'dev'=8] {'grp','dev'}, use_global_device_ids=true, to_apply=%add | all-reduce | flops 32 | bytes 256
  198.8 0.7 constant_dynamic-slice_fusion
  199.5 0.3 select_reduce_fusion
  199.9 0.7 constant_dynamic-slice_fusion.1
  200.6 0.7 reduce_sum.49
  201.3 0.7 dynamic-slice_bitcast_fusion
  201.9 0.2 select_reduce_fusion.1
  202.2 0.2 select_reduce_fusion.2
  202.3 1.2 divide_bitcast_fusion
  203.5 0.6 reduce.16
  204.2 0.6 all_to_all.37.targets
  204.8 0.0 all-to-all-done.6.codes_in
  204.8 1.0 copy-done.1
  205.8 2.7 %shard_map.124 = f32[16,128,128]{2,1,0:T(8,128)} custom-call(s32[32]{0:T(128)} %all_to_all.37.targets, s16[32,128,128]{2,1,0:T(8,128)(2,1)} %copy-done.1, f32[32,1,128]{2,1,0:T(1,128)} %all_to_all.58.scales_in), custom_call_target="tpu_custom_call" | custom-call | tf_op jit(solution)/shard_map/pallas_call | solution.py:180
  (9 shorter events, 0.1 us)
Async XLA Ops:
  9.9 6.1 %copy-start.3 = (s32[64]{0:T(128)S(1)}, s32[64]{0:T(128)}, u32[]{:S(2)}) copy-start(s32[64]{0:T(128)} %param.19) | copy-start | bytes 772
  9.9 53.7 %all-to-all-start.3 = ((bf16[128,128,128]{2,1,0:T(8,128)(2,1)}), bf16[128,128,128]{2,1,0:T(8,128)(2,1)}, u32[]{:S(2)}, u32[]{:S(2)}) async-start(bf16[128,128,128]{2,1,0:T(8,128)(2,1)} %param.11), calls=%async_computation.3 | async-start | bytes 8388608 | tf_op jit(solution)/shard_map/all_to_all | solution.py:153
  63.6 29.5 %all-to-all-start.1 = ((s32[8,8,1]{1,2,0:T(1,128)}), s32[8,8,1]{1,2,0:T(1,128)S(1)}, u32[]{:S(2)}, u32[]{:S(2)}) async-start(s32[8,8,1]{1,2,0:T(1,128)} %bitcast.1), calls=%async_computation.1 | async-start | bytes 8192 | tf_op jit(solution)/shard_map/all_to_all | solution.py:151
  68.4 37.6 %copy-start.4 = (s32[32]{0:T(128)S(1)}, s32[32]{0:T(128)}, u32[]{:S(2)}) copy-start(s32[32]{0:T(128)} %param.20) | copy-start | bytes 388
  100.8 54.5 %copy-start.2 = (f32[8,128]{1,0:T(8,128)S(1)}, f32[8,128]{1,0:T(8,128)}, u32[]{:S(2)}) copy-start(f32[8,128]{1,0:T(8,128)} %param.21) | copy-start | bytes 12292
  100.8 30.3 %all-to-all-start.4 = ((s16[64,128,128]{2,1,0:T(8,128)(2,1)}), s16[64,128,128]{2,1,0:T(8,128)(2,1)S(1)}, u32[]{:S(2)}, u32[]{:S(2)}) async-start(s16[64,128,128]{2,1,0:T(8,128)(2,1)} %get-tuple-element.6), calls=%async_computation.4 | async-start | bytes 4194304 | tf_op jit(solution)/shard_map/all_to_all | solution.py:170
  131.0 4.8 %copy-start = (s16[64,128,128]{2,1,0:T(8,128)(2,1)}, s16[64,128,128]{2,1,0:T(8,128)(2,1)S(1)}, u32[]{:S(2)}) copy-start(s16[64,128,128]{2,1,0:T(8,128)(2,1)S(1)} %all-to-all-done.4.codes_in) | copy-start | bytes 6291460
  131.0 11.6 %all-to-all-start = ((s32[4,8,1]{1,2,0:T(1,128)}), s32[4,8,1]{1,2,0:T(1,128)S(1)}, u32[]{:S(2)}, u32[]{:S(2)}) async-start(s32[4,8,1]{1,2,0:T(1,128)} %bitcast), calls=%async_computation | async-start | bytes 4096 | tf_op jit(solution)/shard_map/all_to_all | solution.py:152
  150.7 54.1 %all-to-all-start.6 = ((s16[32,128,128]{2,1,0:T(8,128)(2,1)}), s16[32,128,128]{2,1,0:T(8,128)(2,1)S(1)}, u32[]{:S(2)}, u32[]{:S(2)}) async-start(s16[32,128,128]{2,1,0:T(8,128)(2,1)} %get-tuple-element.8), calls=%async_computation.6 | async-start | bytes 2097152 | tf_op jit(solution)/shard_map/all_to_all | solution.py:179
  204.8 1.0 copy-start.1

commit v2 on v1

v2 whole, which is shorter than its diff:
```python
import functools
import math

import jax
import jax.numpy as jnp
from jax import lax
from jax.experimental import pallas as pl
from jax.experimental.pallas import tpu as pltpu
from jax.sharding import PartitionSpec as P

LEVELS = 32767.0
TINY = 1e-30
NT = (((1,), (1,)), ((), ()))


def hot(row, width):
    names = lax.broadcasted_iota(jnp.int32, (width, width), 0)
    return (names == row).astype(jnp.bfloat16)


def halves(x):
    high = x.astype(jnp.bfloat16)
    low = (x - high.astype(jnp.float32)).astype(jnp.bfloat16)
    return high, low


def columns(halfway, col):
    width = col.shape[1]
    right = hot(col, width)
    left = jnp.concatenate(halves(halfway), axis=1)
    both = jnp.concatenate([right, right], axis=1)
    return lax.dot_general(left, both, NT, preferred_element_type=jnp.float32)


def project_narrow(block, row, col):
    left = hot(row, row.shape[1])
    return columns(jnp.dot(left, block, preferred_element_type=jnp.float32), col)


def project_wide(block, row, col):
    left = hot(row, row.shape[1])
    both = jnp.concatenate([left, left], axis=1)
    stacked = jnp.concatenate(halves(block), axis=0)
    return columns(jnp.dot(both, stacked, preferred_element_type=jnp.float32), col)


def encode(part):
    peak = jnp.maximum(jnp.max(jnp.abs(part), axis=0, keepdims=True), TINY)
    code = jnp.round(part * (LEVELS / peak)).astype(jnp.int32)
    return code.astype(jnp.int16), peak * (1.0 / LEVELS)


def decode(code, scale):
    return code.astype(jnp.int32).astype(jnp.float32) * scale


def chain(targets, order):
    lanes = targets.shape[1]
    square = (lanes, lanes)
    across = jnp.broadcast_to(targets, square)
    down = across.T
    order_across = jnp.broadcast_to(order, square)
    order_down = order_across.T
    earlier = (across == down) & (order_down < order_across)
    previous = jnp.max(jnp.where(earlier, order_down, -1), axis=0, keepdims=True)
    slots = lax.broadcasted_iota(jnp.int32, square, 1)
    last = jnp.max(jnp.where(down == slots, order_down, -1), axis=0, keepdims=True)
    return previous, last


def coarsen(
    n,
    groups,
    ids_two,
    ids_three,
    blocks,
    labels,
    labels_far,
    weight,
    match_one,
    match_two,
    match_three,
    coarse,
    weight_total,
    land,
    land_labels,
    land_far,
    land_weight,
    near_weight,
    land_weight_far,
    plan,
    plan_smem,
    sums_one,
    out_two,
    out_scale_two,
    land_two,
    land_scale_two,
    sums_two,
    out_three,
    out_scale_three,
    land_three,
    land_scale_three,
    sums_three,
    near_send,
    near_recv,
    far_send,
    far_recv,
    local,
):
    me = lax.axis_index("dev")
    group = lax.axis_index("grp")
    per_one, per_two, per_three = land.shape[1], land_two.shape[1], land_three.shape[1]
    count_one, count_two, count_three = n * per_one, n * per_two, groups * per_three

    def peer(step):
        return lax.rem(me + step, n)

    def source(step):
        return lax.rem(me - step + n, n)

    def far_peer(step):
        return lax.rem(group + step, groups)

    def far_source(step):
        return lax.rem(group - step + groups, groups)

    def near(kind, src, dst, there, here):
        return pltpu.make_async_remote_copy(
            src_ref=src,
            dst_ref=dst,
            send_sem=near_send.at[kind, there],
            recv_sem=near_recv.at[kind, here],
            device_id={"dev": there},
            device_id_type=pl.DeviceIdType.MESH,
        )

    def far(kind, src, dst, there, here):
        return pltpu.make_async_remote_copy(
            src_ref=src,
            dst_ref=dst,
            send_sem=far_send.at[kind, there],
            recv_sem=far_recv.at[kind, here],
            device_id={"grp": there},
            device_id_type=pl.DeviceIdType.MESH,
        )

    def send_labels(v, here):
        return near(0, labels.at[v], land_labels.at[here], v, here)

    def send_weight(v, here):
        return near(1, weight, land_weight.at[here], v, here)

    def send_blocks(v, here):
        return near(2, blocks.at[v], land.at[here], v, here)

    def send_codes(v, here):
        return near(3, out_two.at[v], land_two.at[here], v, here)

    def send_scales(v, here):
        return near(4, out_scale_two.at[v], land_scale_two.at[here], v, here)

    def send_labels_far(v, here):
        return far(0, labels_far.at[v], land_far.at[here], v, here)

    def send_weight_far(v, here):
        return far(1, near_weight, land_weight_far.at[here], v, here)

    def send_codes_far(v, here):
        return far(2, out_three.at[v], land_three.at[here], v, here)

    def send_scales_far(v, here):
        return far(3, out_scale_three.at[v], land_scale_three.at[here], v, here)

    near_kinds = (send_labels, send_weight, send_blocks, send_codes, send_scales)
    far_kinds = (send_labels_far, send_weight_far, send_codes_far, send_scales_far)

    own_blocks = pltpu.make_async_copy(blocks.at[me], land.at[me], local.at[0])
    own_blocks.start()
    own_labels = pltpu.make_async_copy(labels.at[me], land_labels.at[me], local.at[1])
    own_labels.start()
    own_far = pltpu.make_async_copy(labels_far.at[group], land_far.at[group], local.at[2])
    own_far.start()

    barrier = pltpu.get_barrier_semaphore()

    @pl.loop(1, n)
    def _(step):
        pl.semaphore_signal(
            barrier, inc=1, device_id={"dev": peer(step)}, device_id_type=pl.DeviceIdType.MESH
        )

    @pl.loop(1, groups)
    def _(step):
        pl.semaphore_signal(
            barrier, inc=1, device_id={"grp": far_peer(step)}, device_id_type=pl.DeviceIdType.MESH
        )

    pl.semaphore_wait(barrier, n + groups - 2)

    @pl.loop(1, n)
    def _(step):
        send_labels(peer(step), me).start()
        send_weight(peer(step), me).start()

    @pl.loop(1, groups)
    def _(step):
        send_labels_far(far_peer(step), group).start()

    @pl.loop(1, n)
    def _(step):
        send_blocks(peer(step), me).start()

    block_shape = sums_one.shape[1:]
    sums_one[count_one] = jnp.zeros(block_shape, jnp.float32)
    sums_two[count_two] = jnp.zeros(block_shape, jnp.float32)
    sums_three[count_three] = jnp.zeros(block_shape, jnp.float32)

    own_labels.wait()
    own_far.wait()

    @pl.loop(1, n)
    def _(step):
        send_labels(source(step), source(step)).wait_recv()
        send_weight(source(step), source(step)).wait_recv()

    @pl.loop(1, groups)
    def _(step):
        send_labels_far(far_source(step), far_source(step)).wait_recv()

    rows, lanes = plan.shape
    lane = lax.broadcasted_iota(jnp.int32, (rows, lanes), 1)

    def gathered(arrived, sources, per):
        def add(u, held):
            return held + jnp.where(lane // per == u, arrived[u], 0)

        return lax.fori_loop(0, sources, add, jnp.zeros((rows, lanes), jnp.int32))

    lane = lax.broadcasted_iota(jnp.int32, (rows, lanes), 1)
    one_row = lax.broadcasted_iota(jnp.int32, (1, lanes), 1)

    def order(position, sources, per):
        return lax.rem(position - one_row // per + sources, sources) * per + lax.rem(one_row, per)

    known = gathered(land_labels, n, per_one)
    known_two = gathered(land_labels, n, per_two)
    known_far = gathered(land_far, groups, per_three)
    inside_two = one_row < count_two
    inside_three = one_row < count_three
    previous_one, last_one = chain(known[2:3], order(me, n, per_one))
    previous_two, last_two = chain(
        jnp.where(inside_two, known_two[3:4], -1), jnp.where(inside_two, order(me, n, per_two), -1)
    )
    previous_three, last_three = chain(
        jnp.where(inside_three, known_far[0:1], -1),
        jnp.where(inside_three, order(group, groups, per_three), -1),
    )

    def settled(found, zero):
        return jnp.where(found < 0, zero, found)

    plan[0:1] = known[0:1]
    plan[1:2] = known[1:2]
    plan[2:3] = settled(previous_one, count_one)
    plan[3:4] = settled(last_one, count_one)
    plan[4:5] = settled(previous_two, count_two)
    plan[5:6] = settled(last_two, count_two)
    plan[6:7] = settled(previous_three, count_three)
    plan[7:8] = settled(last_three, count_three)
    to_smem = pltpu.make_async_copy(plan, plan_smem, local.at[3])
    to_smem.start()

    held = weight[...]
    for step in range(1, n):
        held = held + land_weight[source(step)]
    near_weight[...] = held
    to_smem.wait()

    def level_one(step):
        u = source(step)
        unroll = math.gcd(per_one, 4)

        @pl.loop(0, per_one // unroll)
        def _(i):
            parts = []
            for j in range(unroll):
                k = i * unroll + j
                row = match_one[pl.ds(plan_smem[0, u * per_one + k], 1), :]
                col = match_one[pl.ds(plan_smem[1, u * per_one + k], 1), :]
                parts.append(project_narrow(land[u, k], row, col))
            for j in range(unroll):
                k = i * unroll + j
                before = sums_one[plan_smem[2, u * per_one + k]]
                sums_one[step * per_one + k] = parts[j] + before

    own_blocks.wait()
    level_one(0)

    @pl.loop(1, n)
    def _(step):
        send_blocks(source(step), source(step)).wait_recv()
        level_one(step)

    def parts_out(v, per, plan_row, ids, table, sums, codes, scales):
        unroll = math.gcd(per, 4)

        @pl.loop(0, per // unroll)
        def _(i):
            parts = []
            for j in range(unroll):
                slot = v * per + i * unroll + j
                row = table[pl.ds(ids[0, slot], 1), :]
                col = table[pl.ds(ids[1, slot], 1), :]
                parts.append(project_wide(sums[plan_smem[plan_row, slot]], row, col))
            for j in range(unroll):
                code, scale = encode(parts[j])
                codes[v, i * unroll + j] = code
                scales[v, i * unroll + j] = scale

    def parts_in(step, u, per, plan_row, codes, scales, sums):
        @pl.loop(0, per)
        def _(k):
            before = sums[plan_smem[plan_row, u * per + k]]
            sums[step * per + k] = decode(codes[u, k], scales[u, k]) + before

    @pl.loop(1, n)
    def _(step):
        v = peer(step)
        parts_out(v, per_two, 3, ids_two, match_two, sums_one, out_two, out_scale_two)
        send_codes(v, me).start()
        send_scales(v, me).start()

    parts_out(me, per_two, 3, ids_two, match_two, sums_one, out_two, out_scale_two)
    parts_in(0, me, per_two, 4, out_two, out_scale_two, sums_two)

    @pl.loop(1, groups)
    def _(step):
        send_weight_far(far_peer(step), group).start()

    @pl.loop(1, n)
    def _(step):
        u = source(step)
        send_codes(u, u).wait_recv()
        send_scales(u, u).wait_recv()
        parts_in(step, u, per_two, 4, land_two, land_scale_two, sums_two)

    @pl.loop(1, groups)
    def _(step):
        v = far_peer(step)
        parts_out(v, per_three, 5, ids_three, match_three, sums_two, out_three, out_scale_three)
        send_codes_far(v, group).start()
        send_scales_far(v, group).start()

    parts_out(group, per_three, 5, ids_three, match_three, sums_two, out_three, out_scale_three)
    parts_in(0, group, per_three, 6, out_three, out_scale_three, sums_three)

    held = near_weight[...]
    for step in range(1, groups):
        send_weight_far(far_source(step), far_source(step)).wait_recv()
        held = held + land_weight_far[far_source(step)]
    weight_total[...] = held

    @pl.loop(1, groups)
    def _(step):
        u = far_source(step)
        send_codes_far(u, u).wait_recv()
        send_scales_far(u, u).wait_recv()
        parts_in(step, u, per_three, 6, land_three, land_scale_three, sums_three)

    @pl.loop(0, coarse.shape[0])
    def _(slot):
        coarse[slot] = sums_three[plan_smem[7, slot]]

    @pl.loop(1, n)
    def _(step):
        for kind in near_kinds:
            kind(peer(step), me).wait_send()

    @pl.loop(1, groups)
    def _(step):
        for kind in far_kinds:
            kind(far_peer(step), group).wait_send()


SMEM = pl.BlockSpec(memory_space=pltpu.SMEM)
VMEM = pl.BlockSpec(memory_space=pltpu.VMEM)
HBM = pl.BlockSpec(memory_space=pl.ANY)
LANES, ROWS = 128, 8


def spread(values, parts, times):
    per = values.shape[0] // parts
    wide = jnp.tile(values.reshape(parts, per), (1, times))
    return jnp.pad(wide, ((0, 0), (0, LANES - times * per)))


def pair_weights(weights, table_rows):
    count, width = weights.shape
    lanes = jnp.arange(width, dtype=jnp.int32)
    match = table_rows.reshape(count // 2, 2 * width)[:, :, None] == lanes
    spread_out = weights.reshape(count // 2, 2 * width)[:, :, None]
    return jnp.sum(jnp.where(match, spread_out, 0.0), axis=1)


def per_device(
    blocks,
    ids_one,
    ids_two,
    ids_three,
    match_one,
    match_two,
    match_three,
    target_one,
    target_two,
    target_three,
    vertex_weights,
):
    n, groups = lax.axis_size("dev"), lax.axis_size("grp")
    count, width = blocks.shape[0], blocks.shape[1]
    rows = [spread(r, n, n) for r in (ids_one[0], ids_one[1], target_one, target_two)]
    labels = jnp.stack(rows + rows, axis=1)
    labels_far = jnp.stack([spread(target_three, groups, groups)] * ROWS, axis=1)
    weight = jnp.broadcast_to(jnp.sum(vertex_weights), (ROWS, LANES))
    per_one, per_two, per_three = count // n, count // 2 // n, count // 4 // groups
    block = (width, width)
    near_kinds, far_kinds = 5, 4
    coarse_graph, total = pl.pallas_call(
        functools.partial(coarsen, n, groups),
        in_specs=[SMEM, SMEM, HBM, VMEM, VMEM, VMEM, VMEM, VMEM, VMEM],
        out_specs=(VMEM, VMEM),
        out_shape=(
            jax.ShapeDtypeStruct((count // 8,) + block, jnp.float32),
            jax.ShapeDtypeStruct((ROWS, LANES), jnp.float32),
        ),
        scratch_shapes=[
            pltpu.VMEM((n, per_one) + block, jnp.bfloat16),
            pltpu.VMEM((n, ROWS, LANES), jnp.int32),
            pltpu.VMEM((groups, ROWS, LANES), jnp.int32),
            pltpu.VMEM((n, ROWS, LANES), jnp.float32),
            pltpu.VMEM((ROWS, LANES), jnp.float32),
            pltpu.VMEM((groups, ROWS, LANES), jnp.float32),
            pltpu.VMEM((ROWS, LANES), jnp.int32),
            pltpu.SMEM((ROWS, LANES), jnp.int32),
            pltpu.VMEM((count + 1,) + block, jnp.float32),
            pltpu.VMEM((n, per_two) + block, jnp.int16),
            pltpu.VMEM((n, per_two, 1, width), jnp.float32),
            pltpu.VMEM((n, per_two) + block, jnp.int16),
            pltpu.VMEM((n, per_two, 1, width), jnp.float32),
            pltpu.VMEM((count // 2 + 1,) + block, jnp.float32),
            pltpu.VMEM((groups, per_three) + block, jnp.int16),
            pltpu.VMEM((groups, per_three, 1, width), jnp.float32),
            pltpu.VMEM((groups, per_three) + block, jnp.int16),
            pltpu.VMEM((groups, per_three, 1, width), jnp.float32),
            pltpu.VMEM((count // 4 + 1,) + block, jnp.float32),
            pltpu.SemaphoreType.DMA((near_kinds, n)),
            pltpu.SemaphoreType.DMA((near_kinds, n)),
            pltpu.SemaphoreType.DMA((far_kinds, groups)),
            pltpu.SemaphoreType.DMA((far_kinds, groups)),
            pltpu.SemaphoreType.DMA((4,)),
        ],
        compiler_params=pltpu.CompilerParams(
            collective_id=0, has_side_effects=True, vmem_limit_bytes=60 * 1024 * 1024
        ),
    )(
        ids_two,
        ids_three,
        blocks.reshape((n, per_one) + block),
        labels,
        labels_far,
        weight,
        match_one,
        match_two,
        match_three,
    )
    owned = vertex_weights.shape[0]
    position = lax.axis_index("grp") * n + lax.axis_index("dev")
    weights = vertex_weights
    for table in (match_one, match_two, match_three):
        mine = lax.dynamic_slice_in_dim(table, position * owned, owned, 0)
        weights = pair_weights(weights, mine)
        owned //= 2
    vertices = weights.shape[0] * n * groups * weights.shape[1]
    return coarse_graph, weights * vertices / total[:1, :1]


def solution(mesh):
    both = ("grp", "dev")
    return jax.shard_map(
        per_device,
        mesh=mesh,
        in_specs=(
            P(both, None, None),
            P(None, both),
            P(None, both),
            P(None, both),
            P(),
            P(),
            P(),
            P(both),
            P(both),
            P(both),
            P(both, None),
        ),
        out_specs=(P(both, None, None), P(both, None)),
        check_vma=False,
    )
```

time: 212 us -> 118 us (0.56); the launches traced: 208 us -> 118 us
  waiting for transfers between devices: 68.9 us -> 0 us
  Pallas kernels: 34.3 us -> 102 us
  blocking collectives: 65.4 us -> 0 us
  starting transfers between devices: 25.4 us -> 0 us
  local copies, waits for them, and re-layouts: 9.33 us -> 12.4 us
    all_to_all x5 -> x0, waiting for transfers between devices: 68.9 us -> none  [the longest x1 46.3 us: per_device(): blocks = swap(blocks, 'dev')]
    pallas_call x3 -> x1, Pallas kernels: 34.3 us -> 102 us  [per_device(): pl.pallas_call(functools.partial(coarsen, n, groups), in_specs=[SMEM, SME...]
    unnamed x1 -> x0, blocking collectives: 42.2 us -> none
    all_to_all x5 -> x0, starting transfers between devices: 25.4 us -> none  [the longest x1 6.07 us: per_device(): blocks = swap(blocks, 'dev')]
    all_to_all x3 -> x0, blocking collectives: 23.2 us -> none  [the longest x1 8 us: per_device(): codes, scales = (swap(codes, 'grp'), swap(scales, 'grp'))]
    all_to_all x7 -> x0, local copies, waits for them, and re-layouts: 3.77 us -> none  [the longest x3 1.83 us: per_device(): arrived_three = swap(target_three, 'grp')]
    another operation x4 -> x17, local copies, waits for them, and re-layouts: 0.9 us -> 4.07 us  [the longest x15 2.79 us: spread(): wide = jnp.tile(values.reshape(parts, per), (1, times))]
  transfers between devices with their start and end apart: 5 -> 0, of which waited for: 2 -> 0; matrix products, arithmetic and copies ran while one was open for 4% -> 0% of each run, Pallas kernels for 15% -> 0%
where the time goes in v2:
time: 118 us
  Pallas kernels  102 us (86%)
  local copies, waits for them, and re-layouts  12.4 us (11%)
  other arithmetic  3.18 us (3%)
    pallas_call x1, Pallas kernels, per_device(): pl.pallas_call(functools.partial(coarsen, n, groups), in_specs=[SMEM, SME...  102 us
    another operation x15, local copies, waits for them, and re-layouts, spread(): wide = jnp.tile(values.reshape(parts, per), (1, times))  2.79 us

profile of v2, /device:TPU:11, one launch (start us, length us, event | category | flops | bytes accessed | tf_op | source)
XLA Modules:
  0.0 117.9 jit_solution(10657662337993432295)
XLA Ops:
  0.6 1.3 %reduce_sum.36 = f32[]{:T(128)} reduce(f32[8,128]{1,0:T(8,128)} %param.21, f32[]{:T(128)} %constant.3.clone.1), dimensions={0,1}, to_apply=%region_0.1 | reduce | flops 1023 | bytes 4104 | tf_op jit(solution)/shard_map/reduce_sum | solution.py:423
  1.9 0.7 dynamic-slice_bitcast_fusion
  2.6 0.8 slice_reduce_fusion
  3.4 0.7 constant_dynamic-slice_fusion.1
  4.1 0.7 tile.62
  4.8 0.1 tile.53
  4.9 0.7 constant_dynamic-slice_fusion
  5.6 1.2 %broadcast_in_dim.48.weight = f32[8,128]{1,0:T(8,128)} broadcast(f32[]{:T(128)} %reduce_sum.36), dimensions={} | broadcast | bytes 4100 | tf_op jit(solution)/shard_map/broadcast_in_dim | solution.py:423
  6.9 0.1 tile.50
  6.9 0.7 tile.56
  7.7 0.7 tile.59
  8.4 0.7 broadcast_in_dim.49
  9.1 0.3 select_reduce_fusion
  9.5 0.2 select_reduce_fusion.1
  9.7 0.2 select_reduce_fusion.2
  9.9 0.1 tile.64
  9.9 0.6 stack.8.labels_far
  10.6 0.1 tile.61
  10.7 0.1 tile.58
  10.7 0.1 tile.52
  10.8 0.1 tile.55
  10.9 0.7 stack.7.labels
  11.6 101.6 %shard_map.122 = (f32[16,128,128]{2,1,0:T(8,128)}, f32[8,128]{1,0:T(8,128)}) custom-call(s32[2,64]{1,0:T(2,128)} %ids_two.1, s32[2,32]{1,0:T(2,128)} %ids_three.1, bf16[8,16,128,128]{3,2,1,0:T(8,128)(2,1)} %bitcast.8, s32[8,8,128]{2,1,0:T(8,128)} %stack.7.labels, s32[4,8,128]{2,1,0:T(8,128)} %stack.8.labels_far, f32[8,128]{1,0:T(8,128)} %broadcast_in_dim.48.weight, ...), custom_call_target="tpu_custom_call" | custom-call | tf_op jit(solution)/shard_map/pallas_call | solution.py:427
  113.2 1.2 %slice.11 = f32[1,1]{1,0:T(1,128)} slice(f32[8,128]{1,0:T(8,128)} %get-tuple-element.5), slice={[0:1], [0:1]} | slice | bytes 8 | tf_op jit(solution)/shard_map/slice | solution.py:483
  114.4 1.2 divide_bitcast_fusion
  115.6 2.3 %copy.14 = f32[16,128,128]{2,1,0:T(8,128)} copy(f32[16,128,128]{2,1,0:T(8,128)} %get-tuple-element.10) | data formatting | bytes 2097152
  (10 shorter events, 0.1 us)

commit v3 on v2

--- a/solution.py
+++ b/solution.py
@@ -54,18 +54,39 @@
     return code.astype(jnp.int32).astype(jnp.float32) * scale
 
 
-def chain(targets, order):
-    lanes = targets.shape[1]
+def fold(weights, row):
+    width = row.shape[1]
+    right = hot(row, width)
+    rest = jnp.broadcast_to(weights, (8, width))
+    total = jnp.zeros((8, width), jnp.float32)
+    for _ in range(3):
+        part = rest.astype(jnp.bfloat16)
+        rest = rest - part.astype(jnp.float32)
+        total = total + lax.dot_general(part, right, NT, preferred_element_type=jnp.float32)
+    return total[:1]
+
+
+def chain(arrived, label, sources, per, mine, lanes):
     square = (lanes, lanes)
-    across = jnp.broadcast_to(targets, square)
-    down = across.T
-    order_across = jnp.broadcast_to(order, square)
-    order_down = order_across.T
-    earlier = (across == down) & (order_down < order_across)
+    count = sources * per
+    down_at = lax.broadcasted_iota(jnp.int32, square, 0)
+    across_at = lax.broadcasted_iota(jnp.int32, square, 1)
+    sender, local_slot = down_at // per, down_at % per
+
+    def add(u, held):
+        row = jnp.broadcast_to(arrived[u, label : label + 1, :], square)
+        return jnp.where(sender == u, row, held)
+
+    held = lax.fori_loop(0, sources, add, jnp.zeros(square, jnp.int32))
+    picked = jnp.where(across_at == mine * per + local_slot, held, 0)
+    down = jnp.broadcast_to(jnp.sum(picked, axis=1, keepdims=True), square)
+    down = jnp.where(down_at < count, down, -1)
+    order_down = (mine - sender + sources) % sources * per + local_slot
+    order_across = (mine - across_at // per + sources) % sources * per + across_at % per
+    earlier = (down.T == down) & (order_down < order_across) & (down_at < count)
     previous = jnp.max(jnp.where(earlier, order_down, -1), axis=0, keepdims=True)
-    slots = lax.broadcasted_iota(jnp.int32, square, 1)
-    last = jnp.max(jnp.where(down == slots, order_down, -1), axis=0, keepdims=True)
-    return previous, last
+    last = jnp.max(jnp.where(down == across_at, order_down, -1), axis=0, keepdims=True)
+    return jnp.where(previous < 0, count, previous), jnp.where(last < 0, count, last)
 
 
 def coarsen(
@@ -75,13 +96,12 @@
     ids_three,
     blocks,
     labels,
-    labels_far,
     weight,
     match_one,
     match_two,
     match_three,
     coarse,
-    weight_total,
+    relative,
     land,
     land_labels,
     land_far,
@@ -90,6 +110,8 @@
     land_weight_far,
     plan,
     plan_smem,
+    labels_smem,
+    coarse_weight,
     sums_one,
     out_two,
     out_scale_two,
@@ -145,7 +167,7 @@
         )
 
     def send_labels(v, here):
-        return near(0, labels.at[v], land_labels.at[here], v, here)
+        return near(0, labels, land_labels.at[here], v, here)
 
     def send_weight(v, here):
         return near(1, weight, land_weight.at[here], v, here)
@@ -160,7 +182,7 @@
         return near(4, out_scale_two.at[v], land_scale_two.at[here], v, here)
 
     def send_labels_far(v, here):
-        return far(0, labels_far.at[v], land_far.at[here], v, here)
+        return far(0, labels, land_far.at[here], v, here)
 
     def send_weight_far(v, here):
         return far(1, near_weight, land_weight_far.at[here], v, here)
@@ -176,9 +198,9 @@
 
     own_blocks = pltpu.make_async_copy(blocks.at[me], land.at[me], local.at[0])
     own_blocks.start()
-    own_labels = pltpu.make_async_copy(labels.at[me], land_labels.at[me], local.at[1])
+    own_labels = pltpu.make_async_copy(labels, land_labels.at[me], local.at[1])
     own_labels.start()
-    own_far = pltpu.make_async_copy(labels_far.at[group], land_far.at[group], local.at[2])
+    own_far = pltpu.make_async_copy(labels, land_far.at[group], local.at[2])
     own_far.start()
 
     barrier = pltpu.get_barrier_semaphore()
@@ -227,53 +249,34 @@
     def _(step):
         send_labels_far(far_source(step), far_source(step)).wait_recv()
 
-    rows, lanes = plan.shape
-    lane = lax.broadcasted_iota(jnp.int32, (rows, lanes), 1)
-
-    def gathered(arrived, sources, per):
-        def add(u, held):
-            return held + jnp.where(lane // per == u, arrived[u], 0)
-
-        return lax.fori_loop(0, sources, add, jnp.zeros((rows, lanes), jnp.int32))
-
-    lane = lax.broadcasted_iota(jnp.int32, (rows, lanes), 1)
-    one_row = lax.broadcasted_iota(jnp.int32, (1, lanes), 1)
-
-    def order(position, sources, per):
-        return lax.rem(position - one_row // per + sources, sources) * per + lax.rem(one_row, per)
-
-    known = gathered(land_labels, n, per_one)
-    known_two = gathered(land_labels, n, per_two)
-    known_far = gathered(land_far, groups, per_three)
-    inside_two = one_row < count_two
-    inside_three = one_row < count_three
-    previous_one, last_one = chain(known[2:3], order(me, n, per_one))
-    previous_two, last_two = chain(
-        jnp.where(inside_two, known_two[3:4], -1), jnp.where(inside_two, order(me, n, per_two), -1)
+    labels_down = pltpu.make_async_copy(land_labels, labels_smem, local.at[4])
+    labels_down.start()
+    lanes = plan.shape[1]
+    levels = (
+        (land_labels, 2, n, per_one, me),
+        (land_labels, 3, n, per_two, me),
+        (land_far, 4, groups, per_three, group),
     )
-    previous_three, last_three = chain(
-        jnp.where(inside_three, known_far[0:1], -1),
-        jnp.where(inside_three, order(group, groups, per_three), -1),
-    )
-
-    def settled(found, zero):
-        return jnp.where(found < 0, zero, found)
-
-    plan[0:1] = known[0:1]
-    plan[1:2] = known[1:2]
-    plan[2:3] = settled(previous_one, count_one)
-    plan[3:4] = settled(last_one, count_one)
-    plan[4:5] = settled(previous_two, count_two)
-    plan[5:6] = settled(last_two, count_two)
-    plan[6:7] = settled(previous_three, count_three)
-    plan[7:8] = settled(last_three, count_three)
+    for level, (arrived, label, sources, per, mine) in enumerate(levels):
+        previous, last = chain(arrived, label, sources, per, mine, lanes)
+        plan[2 * level + 2 : 2 * level + 3] = previous
+        plan[2 * level + 3 : 2 * level + 4] = last
     to_smem = pltpu.make_async_copy(plan, plan_smem, local.at[3])
     to_smem.start()
 
     held = weight[...]
     for step in range(1, n):
-        held = held + land_weight[source(step)]
+        held = held + land_weight[peer(step)]
     near_weight[...] = held
+    position = group * n + me
+    owned = [weight[e : e + 1, :] for e in range(weight.shape[0])]
+    for table in (match_one, match_two, match_three):
+        base = position * len(owned)
+        folded = [fold(w, table[pl.ds(base + e, 1), :]) for e, w in enumerate(owned)]
+        owned = [folded[e] + folded[e + 1] for e in range(0, len(folded), 2)]
+    for e, w in enumerate(owned):
+        coarse_weight[e : e + 1, :] = w
+    labels_down.wait()
     to_smem.wait()
 
     def level_one(step):
@@ -285,8 +288,8 @@
             parts = []
             for j in range(unroll):
                 k = i * unroll + j
-                row = match_one[pl.ds(plan_smem[0, u * per_one + k], 1), :]
-                col = match_one[pl.ds(plan_smem[1, u * per_one + k], 1), :]
+                row = match_one[pl.ds(labels_smem[u, 0, me * per_one + k], 1), :]
+                col = match_one[pl.ds(labels_smem[u, 1, me * per_one + k], 1), :]
                 parts.append(project_narrow(land[u, k], row, col))
             for j in range(unroll):
                 k = i * unroll + j
@@ -358,7 +361,9 @@
     for step in range(1, groups):
         send_weight_far(far_source(step), far_source(step)).wait_recv()
         held = held + land_weight_far[far_source(step)]
-    weight_total[...] = held
+    total = jnp.sum(jnp.sum(held, axis=0, keepdims=True), axis=1, keepdims=True)
+    vertices = relative.shape[0] * n * groups * relative.shape[1]
+    relative[...] = coarse_weight[...] * vertices / total
 
     @pl.loop(1, groups)
     def _(step):
@@ -385,21 +390,7 @@
 SMEM = pl.BlockSpec(memory_space=pltpu.SMEM)
 VMEM = pl.BlockSpec(memory_space=pltpu.VMEM)
 HBM = pl.BlockSpec(memory_space=pl.ANY)
-LANES, ROWS = 128, 8
-
-
-def spread(values, parts, times):
-    per = values.shape[0] // parts
-    wide = jnp.tile(values.reshape(parts, per), (1, times))
-    return jnp.pad(wide, ((0, 0), (0, LANES - times * per)))
-
-
-def pair_weights(weights, table_rows):
-    count, width = weights.shape
-    lanes = jnp.arange(width, dtype=jnp.int32)
-    match = table_rows.reshape(count // 2, 2 * width)[:, :, None] == lanes
-    spread_out = weights.reshape(count // 2, 2 * width)[:, :, None]
-    return jnp.sum(jnp.where(match, spread_out, 0.0), axis=1)
+ROWS = 8
 
 
 def per_device(
@@ -417,30 +408,33 @@
 ):
     n, groups = lax.axis_size("dev"), lax.axis_size("grp")
     count, width = blocks.shape[0], blocks.shape[1]
-    rows = [spread(r, n, n) for r in (ids_one[0], ids_one[1], target_one, target_two)]
-    labels = jnp.stack(rows + rows, axis=1)
-    labels_far = jnp.stack([spread(target_three, groups, groups)] * ROWS, axis=1)
-    weight = jnp.broadcast_to(jnp.sum(vertex_weights), (ROWS, LANES))
+    lanes = -(-count // width) * width
+    rows = (ids_one, target_one[None], target_two[None], target_three[None])
+    held = [jnp.pad(r, ((0, 0), (0, lanes - r.shape[1]))) for r in rows]
+    labels = jnp.pad(jnp.concatenate(held), ((0, ROWS - 5), (0, 0)))
+    owned = vertex_weights.shape[0]
     per_one, per_two, per_three = count // n, count // 2 // n, count // 4 // groups
     block = (width, width)
     near_kinds, far_kinds = 5, 4
-    coarse_graph, total = pl.pallas_call(
+    return pl.pallas_call(
         functools.partial(coarsen, n, groups),
-        in_specs=[SMEM, SMEM, HBM, VMEM, VMEM, VMEM, VMEM, VMEM, VMEM],
+        in_specs=[SMEM, SMEM, HBM, VMEM, VMEM, VMEM, VMEM, VMEM],
         out_specs=(VMEM, VMEM),
         out_shape=(
             jax.ShapeDtypeStruct((count // 8,) + block, jnp.float32),
-            jax.ShapeDtypeStruct((ROWS, LANES), jnp.float32),
+            jax.ShapeDtypeStruct((owned // 8, width), jnp.float32),
         ),
         scratch_shapes=[
             pltpu.VMEM((n, per_one) + block, jnp.bfloat16),
-            pltpu.VMEM((n, ROWS, LANES), jnp.int32),
-            pltpu.VMEM((groups, ROWS, LANES), jnp.int32),
-            pltpu.VMEM((n, ROWS, LANES), jnp.float32),
-            pltpu.VMEM((ROWS, LANES), jnp.float32),
-            pltpu.VMEM((groups, ROWS, LANES), jnp.float32),
-            pltpu.VMEM((ROWS, LANES), jnp.int32),
-            pltpu.SMEM((ROWS, LANES), jnp.int32),
+            pltpu.VMEM((n, ROWS, lanes), jnp.int32),
+            pltpu.VMEM((groups, ROWS, lanes), jnp.int32),
+            pltpu.VMEM((n, owned, width), jnp.float32),
+            pltpu.VMEM((owned, width), jnp.float32),
+            pltpu.VMEM((groups, owned, width), jnp.float32),
+            pltpu.VMEM((ROWS, lanes), jnp.int32),
+            pltpu.SMEM((ROWS, lanes), jnp.int32),
+            pltpu.SMEM((n, ROWS, lanes), jnp.int32),
+            pltpu.VMEM((owned // 8, width), jnp.float32),
             pltpu.VMEM((count + 1,) + block, jnp.float32),
             pltpu.VMEM((n, per_two) + block, jnp.int16),
             pltpu.VMEM((n, per_two, 1, width), jnp.float32),
@@ -456,7 +450,7 @@
             pltpu.SemaphoreType.DMA((near_kinds, n)),
             pltpu.SemaphoreType.DMA((far_kinds, groups)),
             pltpu.SemaphoreType.DMA((far_kinds, groups)),
-            pltpu.SemaphoreType.DMA((4,)),
+            pltpu.SemaphoreType.DMA((5,)),
         ],
         compiler_params=pltpu.CompilerParams(
             collective_id=0, has_side_effects=True, vmem_limit_bytes=60 * 1024 * 1024
@@ -466,21 +460,11 @@
         ids_three,
         blocks.reshape((n, per_one) + block),
         labels,
-        labels_far,
-        weight,
+        vertex_weights,
         match_one,
         match_two,
         match_three,
     )
-    owned = vertex_weights.shape[0]
-    position = lax.axis_index("grp") * n + lax.axis_index("dev")
-    weights = vertex_weights
-    for table in (match_one, match_two, match_three):
-        mine = lax.dynamic_slice_in_dim(table, position * owned, owned, 0)
-        weights = pair_weights(weights, mine)
-        owned //= 2
-    vertices = weights.shape[0] * n * groups * weights.shape[1]
-    return coarse_graph, weights * vertices / total[:1, :1]
 
 
 def solution(mesh):

time: 118 us -> 107 us (0.907)
  local copies, waits for them, and re-layouts: 12.4 us -> 4.01 us
  other arithmetic: 3.18 us -> 0.74 us
    another operation x17 -> x0, local copies, waits for them, and re-layouts: 4.07 us -> none  [the longest x15 2.79 us: spread(): wide = jnp.tile(values.reshape(parts, per), (1, times))]
    reduce_sum x4 -> x0, other arithmetic: 2.01 us -> none  [the longest x1 1.29 us: per_device(): weight = jnp.broadcast_to(jnp.sum(vertex_weights), (ROWS, LANES))]
    slice x2 -> x0, local copies, waits for them, and re-layouts: 1.95 us -> none  [the longest x1 1.18 us: per_device(): return (coarse_graph, weights * vertices / total[:1, :1])]
    broadcast_in_dim x3 -> x0, local copies, waits for them, and re-layouts: 1.95 us -> none  [the longest x1 1.24 us: per_device(): weight = jnp.broadcast_to(jnp.sum(vertex_weights), (ROWS, LANES))]
    dynamic_slice x2 -> x0, local copies, waits for them, and re-layouts: 1.39 us -> none  [per_device(): mine = lax.dynamic_slice_in_dim(table, position * owned, owned, 0)]
    unnamed x1 -> x2, local copies, waits for them, and re-layouts: 2.29 us -> 3.41 us
where the time goes in v3:
time: 107 us
  Pallas kernels  102 us (95%)
  local copies, waits for them, and re-layouts  4.01 us (4%)
    pallas_call x1, Pallas kernels, per_device(): pl.pallas_call(functools.partial(coarsen, n, groups), in_specs=[SMEM, SME...  102 us
    unnamed x2, local copies, waits for them, and re-layouts  3.41 us

profile of v3, /device:TPU:11, one launch (start us, length us, event | category | flops | bytes accessed | tf_op | source)
XLA Modules:
  0.0 107.1 jit_solution(11159819744851514645)
XLA Ops:
  0.6 0.7 pad_add_fusion
  1.4 0.6 pad.14.labels
  2.0 101.7 %shard_map.122 = (f32[16,128,128]{2,1,0:T(8,128)}, f32[1,128]{1,0:T(1,128)}) custom-call(s32[2,64]{1,0:T(2,128)} %ids_two.1, s32[2,32]{1,0:T(2,128)} %ids_three.1, bf16[8,16,128,128]{3,2,1,0:T(8,128)(2,1)} %bitcast.4, s32[8,128]{1,0:T(8,128)} %pad.14.labels, f32[8,128]{1,0:T(8,128)} %weight.1, s32[256,128]{1,0:T(8,128)} %match_one.1, s32[128,128]{1,0:T(8,128)} %match_two.1, ...), custom_call_target="tpu_custom_call" | custom-call | tf_op jit(solution)/shard_map/pallas_call | solution.py:419
  103.7 2.3 %copy.15 = f32[16,128,128]{2,1,0:T(8,128)} copy(f32[16,128,128]{2,1,0:T(8,128)} %get-tuple-element.4) | data formatting | bytes 2097152
  106.0 1.1 %copy.16 = f32[1,128]{1,0:T(1,128)} copy(f32[1,128]{1,0:T(1,128)} %get-tuple-element.5) | data formatting | bytes 1024
